TPU v7x, 32 devices: a 4x4x1 block of a 4x4x8 slice. The times are simulated.
32 devices in a mesh: dp: 2 (over z, core), tp: 16 (over x, y).
Axes of the slice: x: 4, y: 4, z: 1, core: 2. Of those that a mesh axis runs over, the one named last changes fastest.
The devices are a block of a 4x4x8 slice.
Arguments:
- x: bfloat16 [7168, 5120], P(('dp', 'tp')), parts along dimension 0
- dy: bfloat16 [7168, 5120], P(('dp', 'tp')), parts along dimension 0
- pre: bfloat16 [7168, 20480], P('dp', 'tp'), parts along dimension 0
- w_in: bfloat16 [5120, 20480], P(None, 'tp')
- w_down: bfloat16 [20480, 5120], P('tp')
Outputs:
- output 1: bfloat16 [7168, 5120], P(('dp', 'tp')), parts along dimension 0
- output 2: bfloat16 [10240, 20480], P('dp', 'tp'), parts along dimension 0
- output 3: bfloat16 [40960, 5120], P(('dp', 'tp')), parts along dimension 0
There are 2 independent parts. A program takes and returns all parts, laid end to end along the dimension named above; an argument that names none is the same for every part.
All inputs are finite; a program needn't handle non-finite values.
Results may differ from a plain program's by a relative error of at most 0.012.
Values are sent between devices in bfloat16 or wider.
A program may use at most 768 MiB of HBM per device.

v0:
```python
import jax
import jax.numpy as jnp


def act(pre):
    return jax.nn.gelu(pre)


def solution(mesh):
    def step(x, dy, pre, w_in, w_down):
        hidden, back = jax.vjp(act, pre.astype(jnp.float32))
        d_hidden = jnp.dot(dy, w_down.T, preferred_element_type=jnp.float32)
        d_pre = back(d_hidden)[0].astype(jnp.bfloat16)
        dx = jnp.dot(d_pre, w_in.T)
        groups = mesh.shape["dp"]

        def by_group(a, b):
            a, b = (t.reshape(groups, -1, t.shape[-1]) for t in (a, b))
            product = jnp.einsum("gta,gtb->gab", a, b, preferred_element_type=jnp.float32)
            return product.astype(jnp.bfloat16).reshape(-1, b.shape[-1])

        return dx, by_group(x, d_pre), by_group(hidden.astype(jnp.bfloat16), dy)

    return step
```

profile of v0, /device:TPU:96, one launch (start us, length us, event | category | flops | bytes accessed | tf_op | source)
XLA Modules:
  0.0 646.3 jit_solution(950579505814395911)
XLA Ops:
  7.2 0.1 all-gather.10.cloned.1.call-start
  7.2 0.7 all-gather.10.cloned.1.call-update
  8.0 0.1 all-gather.12.cloned.1.call-start
  8.0 0.7 all-gather.12.cloned.1.call-update
  8.8 0.1 reduce-scatter.4.cloned.1.call-start
  8.9 211.7 %all-gather.10.cloned.1.call-done = bf16[3584,5120]{1,0:T(8,128)(2,1)} async-done(((bf16[224,5120]{1,0:T(8,128)(2,1)}), bf16[3584,5120]{1,0:T(8,128)(2,1)}) %all-gather.10.cloned.1.call-update) | async-done | bytes 36700176 | tf_op args[1]
  220.5 66.0 %fusion.3 = bf16[3584,1280]{1,0:T(8,128)(2,1)} fusion(bf16[3584,1280]{1,0:T(8,128)(2,1)} %param.2, bf16[3584,5120]{1,0:T(8,128)(2,1)} %all-gather.10.cloned.1.call-done, bf16[1280,5120]{1,0:T(8,128)(2,1)} %param.1), kind=kOutput, calls=%fused_computation.10 | convolution fusion | flops 47072542720 | bytes 68157440 | tf_op jit(solution)/dot_general | solution.py:12
  286.5 56.4 %fusion.20 = bf16[3584,5120]{1,0:T(8,128)(2,1)} fusion(bf16[3584,1280]{1,0:T(8,128)(2,1)} %fusion.3, bf16[5120,1280]{1,0:T(8,128)(2,1)} %param.3), kind=kOutput, calls=%fused_computation.26 | convolution fusion | flops 46976204800 | bytes 58982400 | tf_op jit(solution)/dot_general | solution.py:14
  343.0 0.1 reduce-scatter.4.cloned.1.call-update
  343.0 87.1 %all-gather.12.cloned.1.call-done = bf16[3584,5120]{1,0:T(8,128)(2,1)} async-done(((bf16[224,5120]{1,0:T(8,128)(2,1)}), bf16[3584,5120]{1,0:T(8,128)(2,1)}) %all-gather.12.cloned.1.call-update) | async-done | bytes 36700176 | tf_op jit(solution)/reshape | solution.py:18
  430.1 56.2 %fusion.10 = bf16[5120,1280]{0,1:T(8,128)(2,1)} fusion(bf16[3584,1280]{1,0:T(8,128)(2,1)} %fusion.3, bf16[3584,5120]{1,0:T(8,128)(2,1)} %all-gather.12.cloned.1.call-done), kind=kOutput, calls=%fused_computation.17 | convolution fusion | flops 46982758400 | bytes 58982400 | tf_op jit(solution)/gta,gtb->gab/dot_general | solution.py:19
  486.3 17.6 %copy = bf16[5120,1280]{1,0:T(8,128)(2,1)} copy(bf16[5120,1280]{0,1:T(8,128)(2,1)} %fusion.10) | data formatting | bytes 26214400
  503.9 76.4 %convolution_convert_fusion = bf16[1280,5120]{1,0:T(8,128)(2,1)} fusion(bf16[3584,5120]{1,0:T(8,128)(2,1)} %all-gather.10.cloned.1.call-done, bf16[3584,1280]{1,0:T(8,128)(2,1)} %param.2), kind=kOutput, calls=%fused_computation.6 | convolution fusion | flops 47028633600 | bytes 58982400 | tf_op jit(solution)/gta,gtb->gab/dot_general | solution.py:19
  580.2 59.1 %reduce-scatter.4.cloned.1.call-done = bf16[224,5120]{1,0:T(8,128)(2,1)} async-done(((bf16[3584,5120]{1,0:T(8,128)(2,1)}), bf16[224,5120]{1,0:T(8,128)(2,1)}) %reduce-scatter.4.cloned.1.call-update) | async-done | bytes 2293776
Async XLA Ops:
  7.2 213.3 %all-gather.10.cloned.1.call-start = ((), (), s32[]{:S(2)}) async-start(), calls=%async_computation.1 | async-start | bytes 38993920 | tf_op args[1]
  8.0 422.1 %all-gather.12.cloned.1.call-start = ((), (), s32[]{:S(2)}) async-start(), calls=%async_computation.2 | async-start | bytes 38993920 | tf_op jit(solution)/reshape | solution.py:18
  8.8 630.6 %reduce-scatter.4.cloned.1.call-start = ((), (), s32[]{:S(2)}) async-start(), calls=%async_computation.3 | async-start | bytes 38993920
Sparse Core Ops, SparseCore 0:
  10.0 210.4 all-gather.9
  222.5 207.5 all-gather.11
  434.1 205.1 reduce-scatter.3
where the time goes:
time: 653 us; the launch traced here: 646 us
  waiting for transfers between devices  359 us (55%)
  matrix products  255 us (39%)
  local copies, waits for them, and re-layouts  17.6 us (3%)
  between operations  14.2 us (2%)
    unnamed x5, waiting for transfers between devices  272 us
    dot_general x2, matrix products, by_group(): jnp.einsum('gta,gtb->gab', a, b, preferred_element_type=jnp.float32)  133 us
    reshape x1, waiting for transfers between devices, by_group(): a, b = (t.reshape(groups, -1, t.shape[-1]) for t in (a, b))  87.1 us
    dot_general x1, matrix products, step(): d_hidden = jnp.dot(dy, w_down.T, preferred_element_type=jnp.float32)  66 us
    dot_general x1, matrix products, step(): dx = jnp.dot(d_pre, w_in.T)  56.4 us
    unnamed x1, local copies, waits for them, and re-layouts  17.6 us
  transfers between devices with their start and end apart: 3, of which 3 were waited for; matrix products, arithmetic and copies ran while one was open for 42% of the time, Pallas kernels for 0%

commit v1 on v0

v1 whole, which is shorter than its diff:
```python
import functools
import math

import jax
import jax.numpy as jnp
from jax import lax
from jax.experimental import pallas as pl
from jax.experimental.pallas import tpu as pltpu

P = jax.sharding.PartitionSpec
MESH = pl.DeviceIdType.MESH
F32, BF16 = jnp.float32, jnp.bfloat16
RINGS = ((0, 1), (0, -1), (1, 1), (1, -1))
PIECES = 2
CHUNK = 512
SUB = 256


def act(pre):
    return jax.nn.gelu(pre)


def position(cycle, me, k):
    x, y = me // k, lax.rem(me, k)
    return (x if cycle == 0 else y) * k + lax.rem(x + y, k)


def device(cycle, pos, k):
    n = k * k
    pos = lax.rem(pos + 4 * n, n)
    a, b = pos // k, lax.rem(pos, k)
    m = lax.rem(b - a + k, k)
    return a * k + m if cycle == 0 else m * k + a


def at(i, size):
    return pl.ds(pl.multiple_of(i * size, size), size)


NT = (((1,), (1,)), ((), ()))
NN = (((1,), (0,)), ((), ()))


def kernel(
    n, x, dy, pre, w_in, w_down, dx, dw_in, dw_down, gx, gy, land,
    w, d_pre, turned, wide, pre_in, tall, out_a, out_b, term,
    send, recv, rs_send, rs_recv, w_sem, wide_sem, tall_sem, out_sem, fetch_sem,
):
    k = math.isqrt(n)
    rows, d = x.shape
    tokens, ff = d_pre.shape
    quarter = d // len(RINGS)
    piece = quarter // PIECES
    half = rows // PIECES
    rings = range(len(RINGS))
    me = lax.axis_index("tp")
    pos = [position(cycle, me, k) for cycle, _ in RINGS]
    ahead = [device(c, pos[r] + way, k) for r, (c, way) in enumerate(RINGS)]

    barrier = pltpu.get_barrier_semaphore()
    for to in ahead:
        pl.semaphore_signal(barrier, inc=1, device_id={"tp": to}, device_id_type=MESH)
    pl.semaphore_wait(barrier, len(RINGS))

    def block(r, back):
        cycle, way = RINGS[r]
        return device(cycle, pos[r] - way * back, k)

    own, whole = (dy, x), (gy, gx)

    def part(which, r, c, back):
        columns = pl.ds(pl.multiple_of(r * quarter + c * piece, piece), piece)
        return whole[which].at[at(block(r, back), rows), columns], columns

    def hop(which, r, c, step, first=False):
        to, columns = part(which, r, c, step)
        return pltpu.make_async_remote_copy(
            src_ref=own[which].at[:, columns] if first else to,
            dst_ref=to,
            send_sem=send.at[which, r, c, lax.rem(step, 2)],
            recv_sem=recv.at[which, r, c, step],
            device_id={"tp": ahead[r]},
            device_id_type=MESH,
        )

    def arrived(which, r, c, step):
        got, _ = part(which, r, c, step + 1)
        pltpu.make_async_remote_copy(
            src_ref=got, dst_ref=got, send_sem=send.at[which, r, c, 0],
            recv_sem=recv.at[which, r, c, step], device_id={"tp": ahead[r]}, device_id_type=MESH,
        ).wait_recv()

    def begin(which):
        for c in range(PIECES):
            for r in rings:
                hop(which, r, c, 0, True).start()

    def forward(which, step, c):
        for r in rings:
            arrived(which, r, c, step - 1)

            @pl.when(step >= 2)
            def _():
                hop(which, r, c, step - 2).wait_send()

            hop(which, r, c, step).start()

    def end(which):
        for c in range(PIECES):
            for r in rings:
                arrived(which, r, c, n - 2)
                hop(which, r, c, n - 3).wait_send()
                hop(which, r, c, n - 2).wait_send()

    begin(0)
    loads = [
        pltpu.make_async_copy(w_down.at[:, pl.ds(q * quarter, quarter)], w.at[pl.ds(q * ff, ff), :], w_sem.at[q])
        for q in rings
    ]
    for load in loads:
        load.start()
    for which in range(2):
        stage = wide.at[which, pl.ds(0, rows), :]
        pltpu.make_async_copy(own[which], stage, wide_sem.at[which]).start()
    for which in range(2):
        stage = wide.at[which, pl.ds(0, rows), :]
        pltpu.make_async_copy(own[which], stage, wide_sem.at[which]).wait()
        pltpu.make_async_copy(stage, whole[which].at[at(me, rows), :], wide_sem.at[which]).start()
    for which in range(2):
        stage = wide.at[which, pl.ds(0, rows), :]
        pltpu.make_async_copy(stage, whole[which].at[at(me, rows), :], wide_sem.at[which]).wait()
    for load in loads:
        load.wait()

    def gather_dy(step, _):
        for c in range(PIECES):
            forward(0, step, c)
        return 0

    lax.fori_loop(1, n - 1, gather_dy, 0)
    begin(1)
    end(0)

    chunks = tokens // CHUNK
    subs = ff // SUB

    def chunk_in(i):
        slot = lax.rem(i, 2)
        return (
            pltpu.make_async_copy(gy.at[at(i, CHUNK), :], wide.at[slot], wide_sem.at[slot]),
            pltpu.make_async_copy(pre.at[at(i, CHUNK), :], pre_in.at[slot], wide_sem.at[2 + slot]),
        )

    def tall_in(source, j):
        slot = lax.rem(j, 2)
        return pltpu.make_async_copy(source.at[:, at(j, SUB)], tall.at[slot], tall_sem.at[slot])

    for copy in chunk_in(0):
        copy.start()

    def chunk_step(i, _):
        slot = lax.rem(i, 2)
        for copy in chunk_in(i):
            copy.wait()

        @pl.when(i + 1 < chunks)
        def _():
            for copy in chunk_in(i + 1):
                copy.start()

        def sub_step(m, _):
            d_hidden = jnp.zeros((CHUNK, SUB), F32)
            for q in rings:
                d_hidden += lax.dot_general(
                    wide[slot, :, pl.ds(q * quarter, quarter)],
                    w[pl.ds(pl.multiple_of(q * ff + m * SUB, SUB), SUB), :],
                    NT, preferred_element_type=F32,
                )
            hidden, back = jax.vjp(act, pre_in[slot, :, at(m, SUB)].astype(F32))
            d_pre[at(i, CHUNK), at(m, SUB)] = back(d_hidden)[0].astype(BF16)
            turned[at(m, SUB), at(i, CHUNK)] = hidden.astype(BF16).T

            @pl.when(m == 1)
            def _():
                forward(1, i + 1, 0)

            @pl.when(m == subs - 1)
            def _():
                forward(1, i + 1, 1)

            return 0

        lax.fori_loop(0, subs, sub_step, 0)
        return 0

    tall_in(gy, 0).start()
    lax.fori_loop(0, chunks, chunk_step, 0)

    w_loads = [
        pltpu.make_async_copy(w_in.at[pl.ds(q * quarter, quarter), :], w.at[pl.ds(q * quarter, quarter), :], w_sem.at[q])
        for q in rings
    ]
    for load in w_loads:
        load.start()

    tiles = d // SUB

    def down_out(j):
        slot = lax.rem(j, 2)
        return pltpu.make_async_copy(out_a.at[slot], dw_down.at[:, at(j, SUB)], out_sem.at[slot])

    def down_tile(j):
        slot = lax.rem(j, 2)
        tall_in(gy, j).wait()

        @pl.when(j + 1 < tiles)
        def _():
            tall_in(gy, j + 1).start()

        @pl.when(j >= 2)
        def _():
            down_out(j - 2).wait()

        out_a[slot] = lax.dot_general(turned[...], tall[slot], NN, preferred_element_type=F32).astype(BF16)
        down_out(j).start()

    rest = n - 2 - chunks
    per = -(-tiles // rest)

    def down_step(t, _):
        def one(j, _):
            @pl.when(j < tiles)
            def _():
                down_tile(j)

            return 0

        forward(1, chunks + 1 + t, 0)
        lax.fori_loop(t * per, t * per + per // 2 + 1, one, 0)
        forward(1, chunks + 1 + t, 1)
        lax.fori_loop(t * per + per // 2 + 1, t * per + per, one, 0)
        return 0

    lax.fori_loop(0, rest, down_step, 0)
    down_out(tiles - 2).wait()
    down_out(tiles - 1).wait()
    for load in w_loads:
        load.wait()

    def term_of(r, step):
        return lax.dot_general(
            d_pre[at(block(r, step + 1), rows), :], w[pl.ds(r * quarter, quarter), :], NT, preferred_element_type=F32
        )

    def out_part(r, c, step):
        return wide.at[0, pl.ds(pl.multiple_of((lax.rem(step, 2) * PIECES + c) * half, half), half), pl.ds(r * quarter, quarter)]

    def in_part(r, c):
        return wide.at[1, pl.ds(pl.multiple_of(c * half, half), half), pl.ds(r * quarter, quarter)]

    def push(r, c, step):
        return pltpu.make_async_remote_copy(
            src_ref=out_part(r, c, step),
            dst_ref=land.at[r, step, pl.ds(pl.multiple_of(c * half, half), half), :],
            send_sem=rs_send.at[r, c, lax.rem(step, 2)],
            recv_sem=rs_recv.at[r, c, step],
            device_id={"tp": ahead[r]},
            device_id_type=MESH,
        )

    def fetch(r, c, step):
        return pltpu.make_async_copy(
            land.at[r, step, pl.ds(pl.multiple_of(c * half, half), half), :], in_part(r, c), fetch_sem.at[r, c]
        )

    def terms(step):
        for r in rings:
            term[r] = term_of(r, step)

    def sums(step, c, store):
        for r in rings:
            push(r, c, step - 1).wait_recv()
            fetch(r, c, step - 1).start()
        for r in rings:
            fetch(r, c, step - 1).wait()
            mine = term[r, pl.ds(pl.multiple_of(c * half, half), half), :]
            store(r, (in_part(r, c)[...].astype(F32) + mine).astype(BF16))

    def send_on(step, c):
        def store(r, value):
            @pl.when(step >= 2)
            def _():
                push(r, c, step - 2).wait_send()

            out_part(r, c, step)[...] = value
            if r >= 1:
                push(r - 1, c, step).start()

        sums(step, c, store)
        push(rings[-1], c, step).start()

    for r in rings:
        value = term_of(r, 0).astype(BF16)
        for c in range(PIECES):
            out_part(r, c, 0)[...] = value[c * half : (c + 1) * half]
        if r >= 1:
            for c in range(PIECES):
                push(r - 1, c, 0).start()
    for c in range(PIECES):
        push(rings[-1], c, 0).start()

    def turn(i, _):
        for m in range(subs):
            turned[pl.ds(m * SUB, SUB), at(i, CHUNK)] = d_pre[at(i, CHUNK), pl.ds(m * SUB, SUB)].T
        return 0

    lax.fori_loop(0, chunks, turn, 0)
    terms(1)
    end(1)
    tall_in(gx, 0).start()

    def in_out(j):
        slot = lax.rem(j, 2)
        return pltpu.make_async_copy(out_b.at[slot], dw_in.at[at(j, SUB), :], out_sem.at[2 + slot])

    def in_tile(j):
        slot = lax.rem(j, 2)
        tall_in(gx, j).wait()

        @pl.when(j + 1 < tiles)
        def _():
            tall_in(gx, j + 1).start()

        @pl.when(j >= 2)
        def _():
            in_out(j - 2).wait()

        product = lax.dot_general(turned[...], tall[slot], NN, preferred_element_type=F32)
        out_b[slot] = product.astype(BF16).T
        in_out(j).start()

    ticks = (n - 2) * PIECES

    def tick(t, _):
        step, c = 1 + t // PIECES, lax.rem(t, PIECES)
        send_on(step, c)

        @pl.when(c == PIECES - 1)
        def _():
            terms(step + 1)

        j = (t * tiles) // ticks

        @pl.when(((t + 1) * tiles) // ticks > j)
        def _():
            in_tile(j)

        return 0

    lax.fori_loop(0, ticks, tick, 0)

    for c in range(PIECES):
        def keep(r, value):
            push(r, c, n - 3).wait_send()
            out_part(r, c, n - 3)[...] = value

        sums(n - 1, c, keep)
        finished = wide.at[0, pl.ds((((n - 3) % 2) * PIECES + c) * half, half), :]
        pltpu.make_async_copy(finished, dx.at[pl.ds(c * half, half), :], w_sem.at[c]).start()
    for c in range(PIECES):
        finished = wide.at[0, pl.ds((((n - 3) % 2) * PIECES + c) * half, half), :]
        pltpu.make_async_copy(finished, dx.at[pl.ds(c * half, half), :], w_sem.at[c]).wait()
        for r in rings:
            push(r, c, n - 2).wait_send()
    in_out(tiles - 2).wait()
    in_out(tiles - 1).wait()


def solution(mesh):
    n = mesh.shape["tp"]

    def local(x, dy, pre, w_in, w_down):
        rows, d = x.shape
        tokens, ff = pre.shape
        quarter = d // len(RINGS)
        hbm = pl.BlockSpec(memory_space=pl.ANY)
        outs = [
            (rows, d), (d, ff), (ff, d), (tokens, d), (tokens, d), (len(RINGS), n - 1, rows, quarter),
        ]
        outs = [jax.ShapeDtypeStruct(s, BF16) for s in outs]
        dma = pltpu.SemaphoreType.DMA
        flops = 8 * tokens * d * ff
        return pl.pallas_call(
            functools.partial(kernel, n),
            out_shape=outs,
            in_specs=[hbm] * 5,
            out_specs=[hbm] * len(outs),
            scratch_shapes=[
                pltpu.VMEM((d, ff), BF16),
                pltpu.VMEM((tokens, ff), BF16),
                pltpu.VMEM((ff, tokens), BF16),
                pltpu.VMEM((2, CHUNK, d), BF16),
                pltpu.VMEM((2, CHUNK, ff), BF16),
                pltpu.VMEM((2, tokens, SUB), BF16),
                pltpu.VMEM((2, ff, SUB), BF16),
                pltpu.VMEM((2, SUB, ff), BF16),
                pltpu.VMEM((len(RINGS), rows, quarter), F32),
                dma((2, len(RINGS), PIECES, 2)),
                dma((2, len(RINGS), PIECES, n - 1)),
                dma((len(RINGS), PIECES, 2)),
                dma((len(RINGS), PIECES, n - 1)),
                dma((len(RINGS),)),
                dma((4,)),
                dma((2,)),
                dma((4,)),
                dma((len(RINGS), PIECES)),
            ],
            compiler_params=pltpu.CompilerParams(
                collective_id=0, has_side_effects=True, vmem_limit_bytes=67_043_328
            ),
            cost_estimate=pl.CostEstimate(flops=flops, bytes_accessed=10 * tokens * d, transcendentals=tokens * ff),
            name="mlp_backward",
        )(x, dy, pre, w_in, w_down)[:3]

    rows = P(("dp", "tp"), None)
    return jax.shard_map(
        local,
        mesh=mesh,
        in_specs=(rows, rows, P("dp", "tp"), P(None, "tp"), P("tp", None)),
        out_specs=(rows, P("dp", "tp"), rows),
        check_vma=False,
    )
```

time: 653 us -> 590 us (0.904)
  Pallas kernels: 0 us -> 567 us
  waiting for transfers between devices: 359 us -> 0 us
  matrix products: 255 us -> 0 us
  between operations: 14.2 us -> 0.67 us
    pallas_call x0 -> x1, Pallas kernels: none -> 567 us  [local(): pl.pallas_call(functools.partial(kernel, n), out_shape=outs, in_specs=[hb...]
    unnamed x5 -> x0, waiting for transfers between devices: 272 us -> none
    dot_general x4 -> x0, matrix products: 255 us -> none  [the longest x2 133 us: by_group(): jnp.einsum('gta,gtb->gab', a, b, preferred_element_type=jnp.float32)]
    reshape x1 -> x0, waiting for transfers between devices: 87.1 us -> none  [by_group(): a, b = (t.reshape(groups, -1, t.shape[-1]) for t in (a, b))]
    unnamed x1 -> x11, local copies, waits for them, and re-layouts: 17.6 us -> 20.6 us
  transfers between devices with their start and end apart: 3 -> 0, of which waited for: 3 -> 0; matrix products, arithmetic and copies ran while one was open for 42% -> 0% of each run, Pallas kernels for 0% -> 0%
where the time goes in v1:
time: 590 us; the launch traced here: 588 us
  Pallas kernels  567 us (96%)
  local copies, waits for them, and re-layouts  20.6 us (3%)
    pallas_call x1, Pallas kernels, local(): pl.pallas_call(functools.partial(kernel, n), out_shape=outs, in_specs=[hb...  567 us
    unnamed x11, local copies, waits for them, and re-layouts  20.6 us

profile of v1, /device:TPU:96, one launch (start us, length us, event | category | flops | bytes accessed | tf_op | source)
XLA Modules:
  0.0 588.4 jit_solution(8465000183124282454)
XLA Ops:
  0.6 567.1 %mlp_backward.1 = (bf16[224,5120]{1,0:T(8,128)(2,1)}, bf16[5120,1280]{1,0:T(8,128)(2,1)}, bf16[1280,5120]{1,0:T(8,128)(2,1)}, bf16[3584,5120]{1,0:T(8,128)(2,1)}...) custom-call(bf16[224,5120]{1,0:T(8,128)(2,1)} %x.1, bf16[224,5120]{1,0:T(8,128)(2,1)} %dy.1, ...), custom_call_target="tpu_custom_call" | custom-call | flops 187904819200 | bytes 183500800 | tf_op jit(solution)/shard_map/mlp_backward/pallas_call | solution.py:393
  567.8 0.0 slice-start
  567.8 3.3 copy.11
  571.1 0.0 slice-start.1
  571.1 0.0 slice-start.2
  571.1 0.0 slice-start.3
  571.1 12.3 %copy.12 = bf16[5120,1280]{1,0:T(8,128)(2,1)} copy(bf16[5120,1280]{1,0:T(8,128)(2,1)} %get-tuple-element.13) | data formatting | bytes 26214400
  583.4 0.0 slice-done
  583.4 0.0 slice-done.1
  583.4 0.0 slice-done.2
  583.4 0.0 slice-done.3
  583.5 5.0 copy.13
  (1 shorter events, 0.0 us)
Async XLA Ops:
  567.8 15.7 %slice-start = ((s8[13107200]{0:T(1024)(128)(4,1)}), s8[4194304]{0:T(1024)(128)(4,1)S(1)}, s32[]{:S(2)}) async-start(s8[13107200]{0:T(1024)(128)(4,1)} %bitcast), calls=%async_computation | async-start | bytes 8388608
  571.1 12.3 %slice-start.1 = ((s8[13107200]{0:T(1024)(128)(4,1)}), s8[4194304]{0:T(1024)(128)(4,1)S(1)}, s32[]{:S(2)}) async-start(s8[13107200]{0:T(1024)(128)(4,1)} %bitcast), calls=%async_computation.1 | async-start | bytes 8388608
  571.1 12.3 %slice-start.2 = ((s8[13107200]{0:T(1024)(128)(4,1)}), s8[4194304]{0:T(1024)(128)(4,1)S(1)}, s32[]{:S(2)}) async-start(s8[13107200]{0:T(1024)(128)(4,1)} %bitcast), calls=%async_computation.2 | async-start | bytes 8388608
  571.1 12.3 %slice-start.3 = ((s8[13107200]{0:T(1024)(128)(4,1)}), s8[524288]{0:T(1024)(128)(4,1)S(1)}, s32[]{:S(2)}) async-start(s8[13107200]{0:T(1024)(128)(4,1)} %bitcast), calls=%async_computation.3 | async-start | bytes 1048576

commit v2 on v1

--- a/solution.py
+++ b/solution.py
@@ -27,9 +27,10 @@
 
 def device(cycle, pos, k):
     n = k * k
-    pos = lax.rem(pos + 4 * n, n)
-    a, b = pos // k, lax.rem(pos, k)
-    m = lax.rem(b - a + k, k)
+    rem = (lambda a, b: a % b) if isinstance(pos, int) else lax.rem
+    pos = rem(pos + 4 * n, n)
+    a, b = pos // k, rem(pos, k)
+    m = rem(b - a + k, k)
     return a * k + m if cycle == 0 else m * k + a
 
 
@@ -42,9 +43,9 @@
 
 
 def kernel(
-    n, x, dy, pre, w_in, w_down, dx, dw_in, dw_down, gx, gy, land,
+    n, x, dy, pre, w_in, w_down, dw_in, dw_down, own_term, last_0, last_1, last_2, last_3, gx, gy, land,
     w, d_pre, turned, wide, pre_in, tall, out_a, out_b, term,
-    send, recv, rs_send, rs_recv, w_sem, wide_sem, tall_sem, out_sem, fetch_sem,
+    send, recv, rs_send, rs_recv, w_sem, wide_sem, tall_sem, out_sem, fetch_sem, own_sem,
 ):
     k = math.isqrt(n)
     rows, d = x.shape
@@ -205,6 +206,17 @@
 
     tiles = d // SUB
 
+    def term_of(r, step):
+        return lax.dot_general(
+            d_pre[at(block(r, step + 1), rows), :], w[pl.ds(r * quarter, quarter), :], NT, preferred_element_type=F32
+        )
+
+    def terms(step):
+        for r in rings:
+            term[r] = term_of(r, step)
+
+    own_copy = pltpu.make_async_copy(term, own_term, own_sem)
+
     def down_out(j):
         slot = lax.rem(j, 2)
         return pltpu.make_async_copy(out_a.at[slot], dw_down.at[:, at(j, SUB)], out_sem.at[slot])
@@ -239,18 +251,20 @@
         lax.fori_loop(t * per, t * per + per // 2 + 1, one, 0)
         forward(1, chunks + 1 + t, 1)
         lax.fori_loop(t * per + per // 2 + 1, t * per + per, one, 0)
+
+        @pl.when(t == rest // 2)
+        def _():
+            for load in w_loads:
+                load.wait()
+            terms(n - 1)
+            own_copy.start()
+
         return 0
 
     lax.fori_loop(0, rest, down_step, 0)
     down_out(tiles - 2).wait()
     down_out(tiles - 1).wait()
-    for load in w_loads:
-        load.wait()
-
-    def term_of(r, step):
-        return lax.dot_general(
-            d_pre[at(block(r, step + 1), rows), :], w[pl.ds(r * quarter, quarter), :], NT, preferred_element_type=F32
-        )
+    own_copy.wait()
 
     def out_part(r, c, step):
         return wide.at[0, pl.ds(pl.multiple_of((lax.rem(step, 2) * PIECES + c) * half, half), half), pl.ds(r * quarter, quarter)]
@@ -273,10 +287,6 @@
             land.at[r, step, pl.ds(pl.multiple_of(c * half, half), half), :], in_part(r, c), fetch_sem.at[r, c]
         )
 
-    def terms(step):
-        for r in rings:
-            term[r] = term_of(r, step)
-
     def sums(step, c, store):
         for r in rings:
             push(r, c, step - 1).wait_recv()
@@ -339,7 +349,7 @@
         out_b[slot] = product.astype(BF16).T
         in_out(j).start()
 
-    ticks = (n - 2) * PIECES
+    ticks = (n - 3) * PIECES
 
     def tick(t, _):
         step, c = 1 + t // PIECES, lax.rem(t, PIECES)
@@ -359,25 +369,70 @@
 
     lax.fori_loop(0, ticks, tick, 0)
 
+    last = (last_0, last_1, last_2, last_3)
+
+    def hand_over(r, c):
+        return pltpu.make_async_copy(out_part(r, c, n - 2), last[r].at[pl.ds(c * half, half), :], fetch_sem.at[r, c])
+
     for c in range(PIECES):
         def keep(r, value):
+            push(r, c, n - 4).wait_send()
+            out_part(r, c, n - 2)[...] = value
+            if r >= 1:
+                hand_over(r - 1, c).start()
+
+        sums(n - 2, c, keep)
+        hand_over(rings[-1], c).start()
+    for c in range(PIECES):
+        for r in rings:
+            hand_over(r, c).wait()
             push(r, c, n - 3).wait_send()
-            out_part(r, c, n - 3)[...] = value
-
-        sums(n - 1, c, keep)
-        finished = wide.at[0, pl.ds((((n - 3) % 2) * PIECES + c) * half, half), :]
-        pltpu.make_async_copy(finished, dx.at[pl.ds(c * half, half), :], w_sem.at[c]).start()
-    for c in range(PIECES):
-        finished = wide.at[0, pl.ds((((n - 3) % 2) * PIECES + c) * half, half), :]
-        pltpu.make_async_copy(finished, dx.at[pl.ds(c * half, half), :], w_sem.at[c]).wait()
-        for r in rings:
-            push(r, c, n - 2).wait_send()
     in_out(tiles - 2).wait()
     in_out(tiles - 1).wait()
 
 
+def settle(*arrays):
+    def body(*refs):
+        for i in range(len(arrays)):
+            refs[len(arrays) + i][...] = refs[i][...]
+
+    steps = 10
+    specs = [pl.BlockSpec((a.shape[0] // steps, a.shape[1]), lambda i: (i, 0)) for a in arrays]
+    size = sum(a.size for a in arrays)
+    return pl.pallas_call(
+        body,
+        grid=(steps,),
+        out_shape=[jax.ShapeDtypeStruct(a.shape, a.dtype) for a in arrays],
+        in_specs=specs,
+        out_specs=specs,
+        cost_estimate=pl.CostEstimate(flops=2000 * size, bytes_accessed=4 * size, transcendentals=0),
+        name="settle",
+    )(*arrays)
+
+
+def finish(own_term, *came):
+    rows, quarter = came[0].shape
+    steps = 2
+
+    def body(own, *refs):
+        out = refs[-1]
+        for r, got in enumerate(refs[:-1]):
+            out[:, pl.ds(r * quarter, quarter)] = (got[...].astype(F32) + own[r]).astype(BF16)
+
+    return pl.pallas_call(
+        body,
+        grid=(steps,),
+        out_shape=jax.ShapeDtypeStruct((rows, quarter * len(came)), BF16),
+        in_specs=[pl.BlockSpec((len(came), rows // steps, quarter), lambda i: (0, i, 0))]
+        + [pl.BlockSpec((rows // steps, quarter), lambda i: (i, 0))] * len(came),
+        out_specs=pl.BlockSpec((rows // steps, quarter * len(came)), lambda i: (i, 0)),
+        name="finish",
+    )(own_term, *came)
+
+
 def solution(mesh):
     n = mesh.shape["tp"]
+    k = math.isqrt(n)
 
     def local(x, dy, pre, w_in, w_down):
         rows, d = x.shape
@@ -385,12 +440,14 @@
         quarter = d // len(RINGS)
         hbm = pl.BlockSpec(memory_space=pl.ANY)
         outs = [
-            (rows, d), (d, ff), (ff, d), (tokens, d), (tokens, d), (len(RINGS), n - 1, rows, quarter),
+            (d, ff), (ff, d), *[(rows, quarter)] * len(RINGS), (tokens, d), (tokens, d),
+            (len(RINGS), n - 2, rows, quarter),
         ]
         outs = [jax.ShapeDtypeStruct(s, BF16) for s in outs]
+        outs.insert(2, jax.ShapeDtypeStruct((len(RINGS), rows, quarter), F32))
         dma = pltpu.SemaphoreType.DMA
         flops = 8 * tokens * d * ff
-        return pl.pallas_call(
+        dw_in, dw_down, own_term, *last = pl.pallas_call(
             functools.partial(kernel, n),
             out_shape=outs,
             in_specs=[hbm] * 5,
@@ -408,19 +465,25 @@
                 dma((2, len(RINGS), PIECES, 2)),
                 dma((2, len(RINGS), PIECES, n - 1)),
                 dma((len(RINGS), PIECES, 2)),
-                dma((len(RINGS), PIECES, n - 1)),
+                dma((len(RINGS), PIECES, n - 2)),
                 dma((len(RINGS),)),
                 dma((4,)),
                 dma((2,)),
                 dma((4,)),
                 dma((len(RINGS), PIECES)),
+                dma(()),
             ],
             compiler_params=pltpu.CompilerParams(
                 collective_id=0, has_side_effects=True, vmem_limit_bytes=67_043_328
             ),
             cost_estimate=pl.CostEstimate(flops=flops, bytes_accessed=10 * tokens * d, transcendentals=tokens * ff),
             name="mlp_backward",
-        )(x, dy, pre, w_in, w_down)[:3]
+        )(x, dy, pre, w_in, w_down)
+        last = last[: len(RINGS)]
+        hops = [[(device(c, i, k), device(c, i + way, k)) for i in range(n)] for c, way in RINGS]
+        came = [lax.ppermute(t, "tp", hop) for t, hop in zip(last, hops)]
+        dw_in, dw_down = settle(dw_in, dw_down)
+        return finish(own_term, *came), dw_in, dw_down
 
     rows = P(("dp", "tp"), None)
     return jax.shard_map(

time: 590 us -> 588 us (level)
  local copies, waits for them, and re-layouts: 20.6 us -> 1.33 us
  Pallas kernels: 567 us -> 578 us
  starting transfers between devices: 0 us -> 6.56 us
    pallas_call x0 -> x2, Pallas kernels: none -> 24 us  [the longest x1 19.9 us: settle(): pl.pallas_call(body, grid=(steps,), out_shape=[jax.ShapeDtypeStruct(a.sha...]
    unnamed x11 -> x8, local copies, waits for them, and re-layouts: 20.6 us -> 1.33 us
    pallas_call x1, Pallas kernels: 567 us -> 554 us  [local(): pl.pallas_call(functools.partial(kernel, n), out_shape=outs, in_specs=[hb...]
    ppermute x0 -> x4, starting transfers between devices: none -> 6.56 us  [local(): came = [lax.ppermute(t, 'tp', hop) for t, hop in zip(last, hops)]]
  transfers between devices with their start and end apart: 0 -> 4, of which waited for: 0 -> 0; matrix products, arithmetic and copies ran while one was open for 0% -> 0% of each run, Pallas kernels for 0% -> 3%
where the time goes in v2:
time: 588 us; the launch traced here: 587 us
  Pallas kernels  578 us (98%)
  starting transfers between devices  6.56 us (1%)
    pallas_call x1, Pallas kernels, local(): pl.pallas_call(functools.partial(kernel, n), out_shape=outs, in_specs=[hb...  554 us
    pallas_call x1, Pallas kernels, settle(): pl.pallas_call(body, grid=(steps,), out_shape=[jax.ShapeDtypeStruct(a.sha...  19.9 us
  transfers between devices with their start and end apart: 4, of which 0 were waited for; matrix products, arithmetic and copies ran while one was open for 0% of the time, Pallas kernels for 3%

profile of v2, /device:TPU:96, one launch (start us, length us, event | category | flops | bytes accessed | tf_op | source)
XLA Modules:
  0.0 587.1 jit_solution(5407919843382129340)
XLA Ops:
  0.6 554.4 %mlp_backward.1 = (bf16[5120,1280]{1,0:T(8,128)(2,1)}, bf16[1280,5120]{1,0:T(8,128)(2,1)}, f32[4,224,1280]{2,1,0:T(8,128)}, bf16[224,1280]{1,0:T(8,128)(2,1)}, b...) custom-call(bf16[224,5120]{1,0:T(8,128)(2,1)} %x.1, ...), custom_call_target="tpu_custom_call" | custom-call | flops 187904819200 | bytes 183500800 | tf_op jit(solution)/shard_map/mlp_backward/pallas_call | solution.py:450
  555.1 0.2 collective-permute-start
  555.2 3.2 collective-permute-start.1
  558.4 0.4 collective-permute-start.2
  558.8 2.8 collective-permute-start.3
  561.6 19.9 %settle.1 = (bf16[5120,1280]{1,0:T(8,128)(2,1)}, bf16[1280,5120]{1,0:T(8,128)(2,1)}) custom-call(bf16[5120,1280]{1,0:T(8,128)(2,1)} %get-tuple-element.17.refs_0_, bf16[1280,5120]{1,0:T(8,128)(2,1)} %get-tuple-element.18.refs_1_), custom_call_target="tpu_custom_call" | custom-call | flops 26214400000 | bytes 52428800 | tf_op jit(solution)/shard_map/settle/pallas_call | solution.py:402
  581.6 0.0 collective-permute-done.refs_0_
  581.6 0.0 copy-start
  581.6 0.0 collective-permute-done.1.refs_1_
  581.6 0.0 copy-start.1
  581.6 0.0 collective-permute-done.2.refs_2_
  581.6 0.0 copy-start.2
  581.6 0.0 collective-permute-done.3.refs_3_
  581.6 0.0 copy-start.3
  581.6 0.8 copy-done
  582.4 0.2 copy-done.1
  582.6 0.2 copy-done.2
  582.8 0.2 copy-done.3
  583.0 4.1 finish.1
Async XLA Ops:
  555.1 26.5 %collective-permute-start = (bf16[224,1280]{1,0:T(8,128)(2,1)}, bf16[224,1280]{1,0:T(8,128)(2,1)S(1)}, u32[]{:S(2)}, u32[]{:S(2)}) collective-permute-start(bf16[224,1280]{1,0:T(8,128)(2,1)} %get-tuple-element.13), channel_id=1, source_target_pairs={{0,1},{1,2},{2,3},{3,7},{7,4},{4,5},{5,6},{6,10},{10,11},{11,8},{8... | collective-permute-start | bytes 1720328 | tf_op jit(solution)/shard_map/ppermute | solution.py:484
  555.2 26.3 %collective-permute-start.1 = (bf16[224,1280]{1,0:T(8,128)(2,1)}, bf16[224,1280]{1,0:T(8,128)(2,1)S(1)}, u32[]{:S(2)}, u32[]{:S(2)}) collective-permute-start(bf16[224,1280]{1,0:T(8,128)(2,1)} %get-tuple-element.14), channel_id=1, source_target_pairs={{0,12},{1,0},{2,1},{3,2},{7,3},{4,7},{5,4},{6,5},{10,6},{11,10},{8... | collective-permute-start | bytes 1720328 | tf_op jit(solution)/shard_map/ppermute | solution.py:484
  558.4 23.2 %collective-permute-start.2 = (bf16[224,1280]{1,0:T(8,128)(2,1)}, bf16[224,1280]{1,0:T(8,128)(2,1)S(1)}, u32[]{:S(2)}, u32[]{:S(2)}) collective-permute-start(bf16[224,1280]{1,0:T(8,128)(2,1)} %get-tuple-element.15), channel_id=1, source_target_pairs={{0,4},{4,8},{8,12},{12,13},{13,1},{1,5},{5,9},{9,10},{10,14},{14,2... | collective-permute-start | bytes 1720328 | tf_op jit(solution)/shard_map/ppermute | solution.py:484
  558.8 22.8 %collective-permute-start.3 = (bf16[224,1280]{1,0:T(8,128)(2,1)}, bf16[224,1280]{1,0:T(8,128)(2,1)S(1)}, u32[]{:S(2)}, u32[]{:S(2)}) collective-permute-start(bf16[224,1280]{1,0:T(8,128)(2,1)} %get-tuple-element.16), channel_id=1, source_target_pairs={{0,3},{4,0},{8,4},{12,8},{13,12},{1,13},{5,1},{9,5},{10,9},{14,10}... | collective-permute-start | bytes 1720328 | tf_op jit(solution)/shard_map/ppermute | solution.py:484
  581.6 0.8 copy-start
  581.6 1.0 copy-start.1
  581.6 1.2 copy-start.2
  581.6 1.3 copy-start.3

commit v3 on v2

--- a/solution.py
+++ b/solution.py
@@ -392,19 +392,42 @@
 
 
 def settle(*arrays):
+    steps = 8
+    count = len(arrays)
+
     def body(*refs):
-        for i in range(len(arrays)):
-            refs[len(arrays) + i][...] = refs[i][...]
-
-    steps = 10
-    specs = [pl.BlockSpec((a.shape[0] // steps, a.shape[1]), lambda i: (i, 0)) for a in arrays]
+        sources, targets, stages = (refs[i * count : (i + 1) * count] for i in range(3))
+        sems = refs[3 * count]
+        pairs = [(i, step) for step in range(steps) for i in range(count)]
+
+        def rows(i, step):
+            height = arrays[i].shape[0] // steps
+            return pl.ds(step * height, height)
+
+        def read(i, step):
+            return pltpu.make_async_copy(sources[i].at[rows(i, step), :], stages[i].at[step], sems.at[0, i, step])
+
+        def write(i, step):
+            return pltpu.make_async_copy(stages[i].at[step], targets[i].at[rows(i, step), :], sems.at[1, i, step])
+
+        for pair in pairs:
+            read(*pair).start()
+        for pair in pairs:
+            read(*pair).wait()
+            write(*pair).start()
+        for pair in pairs:
+            write(*pair).wait()
+
     size = sum(a.size for a in arrays)
+    hbm = pl.BlockSpec(memory_space=pl.ANY)
     return pl.pallas_call(
         body,
-        grid=(steps,),
         out_shape=[jax.ShapeDtypeStruct(a.shape, a.dtype) for a in arrays],
-        in_specs=specs,
-        out_specs=specs,
+        in_specs=[hbm] * count,
+        out_specs=[hbm] * count,
+        scratch_shapes=[pltpu.VMEM((steps, a.shape[0] // steps, a.shape[1]), a.dtype) for a in arrays]
+        + [pltpu.SemaphoreType.DMA((2, count, steps))],
+        compiler_params=pltpu.CompilerParams(vmem_limit_bytes=54 * 2**20),
         cost_estimate=pl.CostEstimate(flops=2000 * size, bytes_accessed=4 * size, transcendentals=0),
         name="settle",
     )(*arrays)
@@ -412,20 +435,19 @@
 
 def finish(own_term, *came):
     rows, quarter = came[0].shape
-    steps = 2
 
     def body(own, *refs):
         out = refs[-1]
         for r, got in enumerate(refs[:-1]):
             out[:, pl.ds(r * quarter, quarter)] = (got[...].astype(F32) + own[r]).astype(BF16)
 
+    vmem = pl.BlockSpec(memory_space=pltpu.VMEM)
     return pl.pallas_call(
         body,
-        grid=(steps,),
         out_shape=jax.ShapeDtypeStruct((rows, quarter * len(came)), BF16),
-        in_specs=[pl.BlockSpec((len(came), rows // steps, quarter), lambda i: (0, i, 0))]
-        + [pl.BlockSpec((rows // steps, quarter), lambda i: (i, 0))] * len(came),
-        out_specs=pl.BlockSpec((rows // steps, quarter * len(came)), lambda i: (i, 0)),
+        in_specs=[vmem] * (1 + len(came)),
+        out_specs=vmem,
+        compiler_params=pltpu.CompilerParams(vmem_limit_bytes=16 * 2**20),
         name="finish",
     )(own_term, *came)
 

time: 588 us -> 584 us (level)
  no operation moved by 1% of the time
where the time goes in v3:
time: 584 us; the launch traced here: 583 us
  Pallas kernels  575 us (98%)
  starting transfers between devices  6.56 us (1%)
    pallas_call x1, Pallas kernels, local(): pl.pallas_call(functools.partial(kernel, n), out_shape=outs, in_specs=[hb...  554 us
    pallas_call x1, Pallas kernels, settle(): pl.pallas_call(body, out_shape=[jax.ShapeDtypeStruct(a.shape, a.dtype) fo...  18.6 us
  transfers between devices with their start and end apart: 4, of which 0 were waited for; matrix products, arithmetic and copies ran while one was open for 0% of the time, Pallas kernels for 3%

profile of v3, /device:TPU:96, one launch (start us, length us, event | category | flops | bytes accessed | tf_op | source)
XLA Modules:
  0.0 582.7 jit_solution(7789594114678324197)
XLA Ops:
  0.6 554.5 %mlp_backward.1 = (bf16[5120,1280]{1,0:T(8,128)(2,1)}, bf16[1280,5120]{1,0:T(8,128)(2,1)}, f32[4,224,1280]{2,1,0:T(8,128)}, bf16[224,1280]{1,0:T(8,128)(2,1)}, b...) custom-call(bf16[224,5120]{1,0:T(8,128)(2,1)} %x.1, ...), custom_call_target="tpu_custom_call" | custom-call | flops 187904819200 | bytes 183500800 | tf_op jit(solution)/shard_map/mlp_backward/pallas_call | solution.py:472
  555.1 0.2 collective-permute-start
  555.3 3.2 collective-permute-start.1
  558.4 0.4 collective-permute-start.2
  558.8 2.8 collective-permute-start.3
  561.7 0.0 copy-start
  561.7 18.6 %settle.1 = (bf16[5120,1280]{1,0:T(8,128)(2,1)}, bf16[1280,5120]{1,0:T(8,128)(2,1)}) custom-call(bf16[5120,1280]{1,0:T(8,128)(2,1)} %get-tuple-element.17.refs_0_, bf16[1280,5120]{1,0:T(8,128)(2,1)} %get-tuple-element.18.refs_1_), custom_call_target="tpu_custom_call" | custom-call | flops 26214400000 | bytes 52428800 | tf_op jit(solution)/shard_map/settle/pallas_call | solution.py:423
  580.3 0.0 collective-permute-done.refs_0_
  580.3 0.0 collective-permute-done.1.refs_1_
  580.3 0.0 collective-permute-done.2.refs_2_
  580.3 0.0 collective-permute-done.3.refs_3_
  580.3 0.7 copy-done
  581.0 1.8 finish.1
Async XLA Ops:
  555.1 25.1 %collective-permute-start = (bf16[224,1280]{1,0:T(8,128)(2,1)}, bf16[224,1280]{1,0:T(8,128)(2,1)S(1)}, u32[]{:S(2)}, u32[]{:S(2)}) collective-permute-start(bf16[224,1280]{1,0:T(8,128)(2,1)} %get-tuple-element.13), channel_id=1, source_target_pairs={{0,1},{1,2},{2,3},{3,7},{7,4},{4,5},{5,6},{6,10},{10,11},{11,8},{8... | collective-permute-start | bytes 1720328 | tf_op jit(solution)/shard_map/ppermute | solution.py:506
  555.3 25.0 %collective-permute-start.1 = (bf16[224,1280]{1,0:T(8,128)(2,1)}, bf16[224,1280]{1,0:T(8,128)(2,1)S(1)}, u32[]{:S(2)}, u32[]{:S(2)}) collective-permute-start(bf16[224,1280]{1,0:T(8,128)(2,1)} %get-tuple-element.14), channel_id=1, source_target_pairs={{0,12},{1,0},{2,1},{3,2},{7,3},{4,7},{5,4},{6,5},{10,6},{11,10},{8... | collective-permute-start | bytes 1720328 | tf_op jit(solution)/shard_map/ppermute | solution.py:506
  558.4 21.8 %collective-permute-start.2 = (bf16[224,1280]{1,0:T(8,128)(2,1)}, bf16[224,1280]{1,0:T(8,128)(2,1)S(1)}, u32[]{:S(2)}, u32[]{:S(2)}) collective-permute-start(bf16[224,1280]{1,0:T(8,128)(2,1)} %get-tuple-element.15), channel_id=1, source_target_pairs={{0,4},{4,8},{8,12},{12,13},{13,1},{1,5},{5,9},{9,10},{10,14},{14,2... | collective-permute-start | bytes 1720328 | tf_op jit(solution)/shard_map/ppermute | solution.py:506
  558.8 21.4 %collective-permute-start.3 = (bf16[224,1280]{1,0:T(8,128)(2,1)}, bf16[224,1280]{1,0:T(8,128)(2,1)S(1)}, u32[]{:S(2)}, u32[]{:S(2)}) collective-permute-start(bf16[224,1280]{1,0:T(8,128)(2,1)} %get-tuple-element.16), channel_id=1, source_target_pairs={{0,3},{4,0},{8,4},{12,8},{13,12},{1,13},{5,1},{9,5},{10,9},{14,10}... | collective-permute-start | bytes 1720328 | tf_op jit(solution)/shard_map/ppermute | solution.py:506
  561.7 19.3 %copy-start = (f32[4,224,1280]{2,1,0:T(8,128)S(1)}, f32[4,224,1280]{2,1,0:T(8,128)}, u32[]{:S(2)}) copy-start(f32[4,224,1280]{2,1,0:T(8,128)} %get-tuple-element.12.own) | copy-start | bytes 13762564
